TPU v7x, 32 devices: a whole 2x2x4 slice. The times are simulated.
32 devices in a mesh: row: 8 (over z, y), col: 4 (over x, core).
Axes of the slice: x: 2, y: 2, z: 4, core: 2. Of those that a mesh axis runs over, the one named last changes fastest.
Arguments:
- tile_seeds: int32 [32, 8, 64, 4], P(None, 'row', None, 'col'), may hold values from 0 to 1073741823
- factors: bfloat16 [32, 1024, 64, 512], P(None, 'row', None, 'col'), may hold values from -0.015625 to 0.015625
- lower_inverse: bfloat16 [4, 16, 512, 8, 1024], P(None, None, 'col', None, 'row'), may hold values from -0.1 to 2
- upper_inverse: bfloat16 [4, 16, 512, 8, 1024], P(None, None, 'col', None, 'row'), may hold values from -0.1 to 2
- right_side: float32 [32, 1024], P(None, 'row'), may hold values from -6 to 6
- first_guess: float32 [64, 512], P(None, 'col'), may hold values from -6 to 6
Outputs:
- solution: float32 [64, 512], P(None, 'col')
- hessenberg: float32 [4, 3], replicated
All inputs are finite; a program needn't handle non-finite values.
Results may differ from a plain program's by a relative error of at most 0.011.
Values may be sent and summed in bfloat16 or wider, within the bound.
No kernel may reach another device: no remote copies, remote signals or barrier semaphores. Data moves between devices by JAX's collectives and lax.ppermute only.
A program may use at most 320 MiB of HBM per device.

v0:
```python
import jax
import jax.numpy as jnp
from jax import lax
from jax.sharding import PartitionSpec as P

ORDER = 32768
SWEEPS = 4
ITERS = 3
DIAG_ORDER = 8192


DIAG_SHIFT = 2.0


def scrambled(tile_seed, flat_index):
    hashed = tile_seed + flat_index * 1640531527
    hashed = hashed ^ hashed >> 16 & 65535
    hashed = hashed * 2146121005
    hashed = hashed ^ hashed >> 15 & 131071
    hashed = hashed * 1779033703
    hashed = hashed ^ hashed >> 16 & 65535
    high_bits = hashed >> 8 & 16777215
    return (high_bits.astype(jnp.float32) - 8388607.5) / 8388608.0


def small_solve(normal_matrix, target):
    factor = jnp.linalg.cholesky(normal_matrix)
    order_small = normal_matrix.shape[0]
    forward = []
    for position in range(order_small):
        partial_value = target[position]
        for earlier in range(position):
            partial_value = partial_value - factor[position, earlier] * forward[earlier]
        forward.append(partial_value / factor[position, position])
    backward = [None] * order_small
    for position in reversed(range(order_small)):
        partial_value = forward[position]
        for after_pos in range(position + 1, order_small):
            partial_value = partial_value - factor[after_pos, position] * backward[after_pos]
        backward[position] = partial_value / factor[position, position]
    return backward


def matrix_part(seed_grid, vector_col, row_index, col_index, n_row, n_col):
    tile_size = vector_col.shape[1]
    offsets = jnp.arange(tile_size, dtype=jnp.int32)
    flat_index = offsets[:, None] * tile_size + offsets[None, :]
    col_tiles = jnp.arange(seed_grid.shape[1], dtype=jnp.int32)
    col_ids = (col_tiles[:, None] * n_col + col_index) * tile_size + offsets[None, :]
    entry_scale = ORDER ** (-0.5)

    def one_row(inputs):
        seed_row, tile_row = inputs
        values = scrambled(seed_row[None, :, None], flat_index[:, None, :]) * entry_scale
        row_ids = (tile_row * n_row + row_index) * tile_size + offsets
        values = values + jnp.where(row_ids[:, None, None] == col_ids[None, :, :], DIAG_SHIFT, 0.0)
        return jnp.einsum("icj,cj->i", values, vector_col, precision=lax.Precision.HIGHEST)

    return lax.map(one_row, (seed_grid, jnp.arange(seed_grid.shape[0], dtype=jnp.int32)))


def lower_sweep(vector_row, factors, lower_inverse, row_span, col_span):
    solved = []
    for sweep_step in range(SWEEPS):
        first_row = sweep_step * row_span
        target = vector_row[first_row : first_row + row_span]
        if sweep_step > 0:
            earlier = jnp.concatenate(solved, axis=0).astype(jnp.bfloat16)
            coupled = jnp.einsum(
                "minj,nj->mi",
                factors[first_row : first_row + row_span, :, : sweep_step * col_span, :],
                earlier,
                preferred_element_type=jnp.float32,
            )
            target = target - lax.psum(coupled, "col")
        mapped = jnp.einsum(
            "cimj,mj->ci",
            lower_inverse[sweep_step],
            target.astype(jnp.bfloat16),
            preferred_element_type=jnp.float32,
        )
        solved.append(lax.psum(mapped, "row"))
    return jnp.concatenate(solved, axis=0)


def upper_sweep(own_rows, factors, upper_inverse, row_span, col_span):
    solved = [None] * SWEEPS
    for sweep_step in reversed(range(SWEEPS)):
        first_row = sweep_step * row_span
        next_col = (sweep_step + 1) * col_span
        own_part = own_rows[first_row : first_row + row_span]
        if sweep_step < SWEEPS - 1:
            later_part = jnp.concatenate(solved[sweep_step + 1 :], axis=0).astype(jnp.bfloat16)
            coupled = jnp.einsum(
                "minj,nj->mi",
                factors[first_row : first_row + row_span, :, next_col:, :],
                later_part,
                preferred_element_type=jnp.float32,
            )
            sent = -coupled
            target = (own_part + lax.psum(sent, "col")).astype(jnp.bfloat16)
        else:
            target = own_part.astype(jnp.bfloat16)
        mapped = jnp.einsum(
            "cimj,mj->ci", upper_inverse[sweep_step], target, preferred_element_type=jnp.float32
        )
        solved[sweep_step] = lax.psum(mapped, "row")
    return jnp.concatenate(solved, axis=0)


def shards(tile_seeds, factors, lower_inverse, upper_inverse, right_side, first_guess):
    n_row = lax.axis_size("row")
    n_col = lax.axis_size("col")
    row_index = lax.axis_index("row")
    col_index = lax.axis_index("col")
    seed_grid = tile_seeds[:, 0, :, 0]
    tile_size = right_side.shape[1]
    row_span = DIAG_ORDER // (tile_size * n_row)
    col_span = DIAG_ORDER // (tile_size * n_col)

    def apply_system(vector_col):
        partial_value = matrix_part(seed_grid, vector_col, row_index, col_index, n_row, n_col)
        return lax.psum(partial_value, "col")

    residual = right_side - apply_system(first_guess)
    initial_norm = jnp.sqrt(lax.psum(jnp.sum(residual * residual), "row"))
    basis_list = [residual / initial_norm]
    directions = []
    hessenberg = jnp.zeros((ITERS + 1, ITERS), jnp.float32)
    for column in range(ITERS):
        lowered = lower_sweep(basis_list[column], factors, lower_inverse, row_span, col_span)
        gathered = lax.all_gather(lowered, "col", axis=1, tiled=True)
        spread = gathered.reshape(-1, n_row, tile_size)
        own_rows = lax.dynamic_index_in_dim(spread, row_index, 1, keepdims=False)
        direction = upper_sweep(own_rows, factors, upper_inverse, row_span, col_span)
        directions.append(direction)
        mapped = apply_system(direction)
        stacked = jnp.stack(basis_list)
        coeffs, squared = lax.psum(
            (jnp.sum(stacked * mapped[None], axis=(1, 2)), jnp.sum(mapped * mapped)), "row"
        )
        mapped = mapped - jnp.sum(coeffs[:, None, None] * stacked, axis=0)
        length = jnp.sqrt(squared - jnp.sum(coeffs * coeffs))
        hessenberg = (
            hessenberg.at[: column + 1, column].set(coeffs).at[column + 1, column].set(length)
        )
        if column + 1 < ITERS:
            basis_list.append(mapped / length)
    normal_matrix = jnp.dot(hessenberg.T, hessenberg, precision=lax.Precision.HIGHEST)
    weights = small_solve(normal_matrix, initial_norm * hessenberg[0])
    solution = first_guess
    for position in range(ITERS):
        solution = solution + weights[position] * directions[position]
    return (solution, hessenberg)


def solution(mesh):
    in_specs = (
        P(None, "row", None, "col"),
        P(None, "row", None, "col"),
        P(None, None, "col", None, "row"),
        P(None, None, "col", None, "row"),
        P(None, "row"),
        P(None, "col"),
    )
    out_specs = (P(None, "col"), P())
    return jax.shard_map(shards, mesh=mesh, in_specs=in_specs, out_specs=out_specs, check_vma=False)
```

profile of v0, /device:TPU:0, one launch (start us, length us, event | category | flops | bytes accessed | tf_op | source)
XLA Modules:
  0.0 2343.3 jit_solution(12727246034049527136)
XLA Ops:
  0.7 321.6 %while.58 = (s32[]{:T(128)}, f32[32,128]{1,0:T(8,128)S(1)}, s32[32,64]{1,0:T(8,128)}, s32[32]{0:T(128)S(1)}, s32[]{:T(128)}, /*index=5*/f32[64,128]{1,0:T(8,128)...) while((s32[]{:T(128)}, f32[32,128]{1,0:T(8,128)S(1)}, ...), condition=%wide.region_1.2_spmd.clone, body=%wide.region_0.1_spmd.clone.sunk | while | flops 33595524 | bytes 8753357 | solution.py:59
  322.3 12.7 psum.371
  335.6 22.3 psum.372
  358.6 12.3 slice_bitcast_fusion.7
  370.9 6.8 copy.23
  380.6 17.4 psum.373
  413.9 17.8 psum.374
  431.7 6.8 copy.29
  441.4 19.4 psum.375
  460.8 12.7 fusion.190
  473.4 12.7 copy.32
  506.1 17.4 psum.377
  523.5 18.5 fusion.192
  542.0 17.7 copy.38
  580.5 19.4 psum.379
  605.4 12.2 slice_bitcast_fusion.1
  617.6 6.8 copy.44
  627.2 17.4 psum.380
  669.6 19.4 psum.382
  689.0 12.7 copy.53
  721.7 17.4 psum.384
  739.1 17.7 copy.59
  777.8 19.8 psum.386
  797.6 316.5 %while.59 = (s32[]{:T(128)}, f32[32,128]{1,0:T(8,128)S(1)}, s32[32,64]{1,0:T(8,128)}, s32[32]{0:T(128)S(1)}, s32[]{:T(128)}, /*index=5*/f32[64,128]{1,0:T(8,128)...) while((s32[]{:T(128)}, f32[32,128]{1,0:T(8,128)S(1)}, ...), condition=%wide.region_20.21_spmd.clone, body=%wide.region_19.20_spmd.clone.sunk | while | flops 33595524 | bytes 8622257 | solution.py:59
  1114.1 10.1 psum.387
  1124.8 17.8 all-reduce.3
  1148.0 19.4 psum.390
  1178.9 17.4 psum.392
  1209.4 19.5 psum.394
  1243.2 17.4 psum.396
  1268.8 19.4 psum.397
  1299.7 17.4 psum.399
  1330.3 19.4 psum.401
  1363.9 17.6 psum.403
  1381.5 317.2 %while.60 = (s32[]{:T(128)}, f32[32,128]{1,0:T(8,128)S(1)}, s32[32,64]{1,0:T(8,128)}, s32[32]{0:T(128)S(1)}, s32[]{:T(128)}, /*index=5*/f32[64,128]{1,0:T(8,128)...) while((s32[]{:T(128)}, f32[32,128]{1,0:T(8,128)S(1)}, ...), condition=%wide.region_42.43_spmd.clone, body=%wide.region_41.42_spmd.clone.sunk | while | flops 33595524 | bytes 8622257 | solution.py:59
  1698.7 10.1 psum.404
  1709.5 19.8 all-reduce.2
  1734.2 17.4 psum.407
  1763.0 19.3 psum.409
  1795.5 17.8 psum.411
  1827.6 19.3 psum.413
  1855.2 17.4 psum.414
  1884.1 19.3 psum.416
  1916.6 17.4 psum.418
  1948.2 19.5 psum.420
  1967.8 320.8 %while.61 = (s32[]{:T(128)}, f32[32,128]{1,0:T(8,128)S(1)}, s32[32,64]{1,0:T(8,128)}, s32[32]{0:T(128)S(1)}, s32[]{:T(128)}, /*index=5*/f32[64,128]{1,0:T(8,128)...) while((s32[]{:T(128)}, f32[32,128]{1,0:T(8,128)S(1)}, ...), condition=%wide.region_66.67_spmd.clone, body=%wide.region_65.66_spmd.clone.sunk | while | flops 33595524 | bytes 8622257 | solution.py:59
  2288.6 10.1 psum.421
  2299.4 17.8 all-reduce.1
  (1300 shorter events, 1517.0 us)
Async XLA Ops:
  0.7 334.3 %copy-start.2 = (f32[32,128]{1,0:T(8,128)S(1)}, f32[32,128]{1,0:T(8,128)}, u32[]{:S(2)}) copy-start(f32[32,128]{1,0:T(8,128)} %param.30) | copy-start | bytes 49156
  0.7 4.7 copy-start
  10.8 4.7 copy-start
  20.8 4.7 copy-start
  30.9 4.7 copy-start
  40.9 4.7 copy-start
  50.9 4.7 copy-start
  61.0 4.7 copy-start
  71.0 4.7 copy-start
  81.1 4.7 copy-start
  91.1 4.7 copy-start
  101.2 4.7 copy-start
  111.2 4.7 copy-start
  121.3 4.7 copy-start
  131.3 4.7 copy-start
  141.4 4.7 copy-start
  151.4 4.7 copy-start
  161.5 4.7 copy-start
  171.5 4.7 copy-start
  181.6 4.7 copy-start
  191.6 4.7 copy-start
  201.7 4.7 copy-start
  211.7 4.7 copy-start
  221.8 4.7 copy-start
  231.8 4.7 copy-start
  241.9 4.7 copy-start
  251.9 4.7 copy-start
  262.0 4.7 copy-start
  272.0 4.7 copy-start
  282.1 4.7 copy-start
  292.1 4.7 copy-start
  302.2 4.7 copy-start
  312.2 4.7 copy-start
  1967.8 357.4 %copy-start.3 = (s32[2]{0:T(128)S(1)}, s32[2]{0:T(128)}, u32[]{:S(2)}) copy-start(s32[2]{0:T(128)} %constant.590.clone.1) | copy-start | bytes 28
  1967.8 374.0 %copy-start.1 = (f32[64,128]{1,0:T(8,128)S(1)}, f32[64,128]{1,0:T(8,128)}, u32[]{:S(2)}) copy-start(f32[64,128]{1,0:T(8,128)} %get-tuple-element.1081) | copy-start | bytes 98308
where the time goes:
time: 2360 us; the launch traced here: 2340 us
  matrix products  827 us (35%)
  blocking collectives  695 us (29%)
  local copies, waits for them, and re-layouts  372 us (16%)
  other arithmetic  341 us (14%)
  loops' own time  92.1 us (4%)
    dot_general x128, matrix products, one_row(): jnp.einsum('icj,cj->i', values, vector_col, precision=lax.Precision.HIGHEST)  681 us
    add x128, other arithmetic, one_row(): values + jnp.where(row_ids[:, None, None] == col_ids[None, :, :], DIAG_SH...  309 us
    psum x12, blocking collectives, upper_sweep(): solved[sweep_step] = lax.psum(mapped, 'row')  221 us
    psum x12, blocking collectives, lower_sweep(): solved.append(lax.psum(mapped, 'row'))  221 us
    another operation x4, loops' own time, matrix_part(): lax.map(one_row, (seed_grid, jnp.arange(seed_grid.shape[0], dtype=jnp.int...  92.1 us
    add x128, local copies, waits for them, and re-layouts, scrambled(): hashed = tile_seed + flat_index * 1640531527  89.3 us
    dynamic_slice x128, local copies, waits for them, and re-layouts, matrix_part(): lax.map(one_row, (seed_grid, jnp.arange(seed_grid.shape[0], dtype=jnp.int...  81.4 us
    slice x6, local copies, waits for them, and re-layouts, upper_sweep(): factors[first_row:first_row + row_span, :, next_col:, :]  74.7 us

commit v1 on v0

v1 whole, which is shorter than its diff:
```python
import functools

import jax
import jax.numpy as jnp
from jax import lax
from jax.experimental import pallas as pl
from jax.experimental.pallas import tpu as pltpu
from jax.sharding import PartitionSpec as P

ITERS = 3
DIAG_SHIFT = 2.0
F32 = jnp.float32
BF16 = jnp.bfloat16
LANES = 128
NT = (((1,), (1,)), ((), ()))
VMEM_LIMIT = 24 << 20
COST_RATE = 5e8


def split_rows(row):
    wide = jnp.broadcast_to(row, (16, row.shape[1]))
    high = wide.astype(BF16).astype(F32)
    at = lax.broadcasted_iota(jnp.int32, wide.shape, 0)
    return jnp.where(at == 0, high, jnp.where(at == 1, wide - high, 0.0)).astype(BF16)


def hashed(seed, step):
    h = seed + step
    h = h ^ lax.shift_right_logical(h, 16)
    h = h * 2146121005
    h = h ^ lax.shift_right_logical(h, 15)
    h = h * 1779033703
    h = h ^ lax.shift_right_logical(h, 16)
    return h ^ jnp.int32(-2147483648)


def generate_body(n_rows, seeds, table, x_ref, a_ref, y_ref):
    step = pl.program_id(0)

    @pl.when(step == 0)
    def _():
        y_ref[...] = jnp.zeros_like(y_ref)

    def tiles(at, carry):
        for half in range(2):
            m = 2 * at + half
            for q in range(2):
                seed = seeds[m, 2 * step + q]
                for part in range(4):
                    rows = pl.ds(part * 32, 32)
                    h = hashed(seed, table[rows, :])
                    a_ref[pl.ds(q * LANES + part * 32, 32), pl.ds(m * LANES, LANES)] = h.astype(F32).astype(BF16)
        return carry

    lax.fori_loop(0, n_rows // 2, tiles, 0)
    left = jnp.concatenate([split_rows(x_ref[pl.ds(2 * step + q, 1), :]) for q in range(2)], axis=1)
    y_ref[...] += jnp.dot(left, a_ref[...], preferred_element_type=F32)


def generate(seeds, table, x_col):
    n_rows, n_cols = seeds.shape
    wide = n_rows * LANES
    return pl.pallas_call(
        functools.partial(generate_body, n_rows),
        grid=(n_cols // 2,),
        in_specs=[
            pl.BlockSpec(memory_space=pltpu.SMEM),
            pl.BlockSpec((LANES, LANES), lambda g: (0, 0)),
            pl.BlockSpec((n_cols, LANES), lambda g: (0, 0)),
        ],
        out_specs=[
            pl.BlockSpec((2 * LANES, wide), lambda g: (g, 0)),
            pl.BlockSpec((16, wide), lambda g: (0, 0)),
        ],
        out_shape=[
            jax.ShapeDtypeStruct((n_cols * LANES, wide), BF16),
            jax.ShapeDtypeStruct((16, wide), F32),
        ],
        compiler_params=pltpu.CompilerParams(vmem_limit_bytes=32 << 20),
        name="generate",
    )(seeds, table, x_col)


def cost(micros):
    return pl.CostEstimate(flops=int(micros * COST_RATE), bytes_accessed=int(micros * 3e6), transcendentals=0)


def vmem_spec():
    return pl.BlockSpec(memory_space=pltpu.VMEM)


def fetched(refs, buffers, sem):
    copies = [pltpu.make_async_copy(ref, buffer, sem.at[at]) for at, (ref, buffer) in enumerate(zip(refs, buffers))]
    for copy in copies:
        copy.start()
    return copies


def small_scratch(smalls):
    return [pltpu.VMEM(x.shape, x.dtype) for x in smalls] + [pltpu.SemaphoreType.DMA((len(smalls),))]


def any_spec():
    return pl.BlockSpec(memory_space=pl.ANY)


def apply_body(steps, first, slots, scale, last, n_small, place, *refs):
    smalls, a_ref, y_ref = refs[:n_small], refs[n_small], refs[n_small + 1]
    buffers, small_sem = refs[n_small + 2 : 2 * n_small + 2], refs[2 * n_small + 2]
    acc, z_all, held, sems = refs[2 * n_small + 3 :]
    chunk = held.shape[1]
    tiles = chunk // LANES

    def copy(at):
        slot = lax.rem(at, slots)
        return pltpu.make_async_copy(a_ref.at[pl.ds((first * steps + at) * chunk, chunk), :], held.at[slot], sems.at[slot])

    waits = fetched(smalls, buffers, small_sem)
    for at in range(min(slots - 1, steps)):
        copy(at).start()
    for wait in waits:
        wait.wait()
    z_ref, rest = buffers[0], buffers[1:]
    if first < last:
        acc[...] = rest[0][...]
        rest = rest[1:]
    else:
        acc[...] = jnp.zeros_like(acc)
    z_all[...] = jnp.sum(z_ref[...], axis=0)

    def body(at, carry):
        @pl.when(at + slots - 1 < steps)
        def _():
            copy(at + slots - 1).start()

        left = jnp.concatenate([split_rows(z_all[pl.ds(tiles * at + q, 1), :]) for q in range(tiles)], axis=1)
        copy(at).wait()
        acc[...] += jnp.dot(left, held[lax.rem(at, slots)], preferred_element_type=F32)
        return carry

    lax.fori_loop(0, steps, body, 0)
    if first > 0:
        y_ref[...] = acc[...]
        return
    total = acc[0:1, :] + acc[1:2, :]
    for m in range(y_ref.shape[0]):
        y_ref[m : m + 1, :] = total[:, m * LANES : (m + 1) * LANES] * scale
    count = y_ref.shape[0] // (last + 1)
    spread = z_all.shape[0] // count
    for at, ref in enumerate(rest):
        y_ref[(at + 1) * count : (at + 2) * count, :] += DIAG_SHIFT * ref[...]
    mine = z_all[pl.ds(place[0], count, stride=spread), :]
    y_ref[0:count, :] += jnp.where(place[1] == 1, DIAG_SHIFT, 0.0) * mine


def apply_block(a, parts, block, blocks, prior, owns, place, scale):
    depth, wide = a.shape
    span = depth // blocks
    chunk = min(256, span)
    slots = min(8, span // chunk)
    smalls = [parts] + prior + owns
    return pl.pallas_call(
        functools.partial(apply_body, span // chunk, block, slots, scale, blocks - 1, len(smalls)),
        in_specs=[pl.BlockSpec(memory_space=pltpu.SMEM)] + [any_spec()] * (len(smalls) + 1),
        out_specs=vmem_spec(),
        out_shape=jax.ShapeDtypeStruct((wide // LANES, LANES) if block == 0 else (16, wide), F32),
        scratch_shapes=small_scratch(smalls)
        + [
            pltpu.VMEM((16, wide), F32),
            pltpu.VMEM(parts.shape[1:], F32),
            pltpu.VMEM((slots, chunk, wide), BF16),
            pltpu.SemaphoreType.DMA((slots,)),
        ],
        compiler_params=pltpu.CompilerParams(vmem_limit_bytes=VMEM_LIMIT),
        cost_estimate=cost(6.0),
        name="apply_block",
    )(place, *smalls, a)


def rows_body(count, n, source, n_small, prepare, finish, *refs):
    operands, w_ref, out_ref = refs[:n_small], refs[n_small], refs[n_small + 1]
    smalls, small_sem = refs[n_small + 2 : 2 * n_small + 2], refs[2 * n_small + 2]
    scratch_a, scratch_b, totals = refs[2 * n_small + 3 : 2 * n_small + 6]
    group = min(n, 8)
    chunk = 16
    waits = fetched(operands, smalls, small_sem)
    near = len(refs) == 2 * n_small + 6
    if near:
        held = w_ref
    else:
        held, sems = refs[2 * n_small + 6 :]

        def copy(at):
            return pltpu.make_async_copy(source(w_ref, at), held.at[at], sems.at[at])

        for at in range(count):
            copy(at).start()
    for wait in waits:
        wait.wait()
    vec = prepare(*smalls)

    def multiply(at, scratch):
        if not near:
            copy(at).wait()
        for part in range(LANES // chunk):
            if len(held.shape) == 3:
                w = held[at, pl.ds(part * chunk * n, chunk * n), :].astype(F32).reshape(chunk, n, LANES)
            else:
                w = held[at, pl.ds(part * chunk, chunk), :, :].astype(F32)
            p = w * vec[None]
            if n > 8:
                p = jnp.sum(p.reshape(chunk, n // 8, 8, LANES), axis=1)
            scratch[pl.ds(part * chunk * group, chunk * group), :] = p.reshape(chunk * group, LANES)

    def add_up(at, scratch):
        total = scratch[pl.ds(0, LANES, stride=group), :]
        for q in range(1, group):
            total = total + scratch[pl.ds(q, LANES, stride=group), :]
        high = total.astype(BF16)
        at = pl.ds(at * LANES, LANES)
        totals[at, 0:LANES] = high
        totals[at, LANES : 2 * LANES] = (total - high.astype(F32)).astype(BF16)

    def body(at, carry):
        multiply(2 * at, scratch_a)

        @pl.when(at > 0)
        def _():
            add_up(2 * at - 1, scratch_b)

        multiply(2 * at + 1, scratch_b)
        add_up(2 * at, scratch_a)
        return carry

    lax.fori_loop(0, count // 2, body, 0)
    add_up(count - 1, scratch_b)
    ones = jnp.ones((16, 2 * LANES), BF16)
    out = lax.dot_general(ones, totals[...], NT, preferred_element_type=F32)
    finish(out_ref, [out[0:1, at * LANES : (at + 1) * LANES] for at in range(count)], *smalls)


def rows_product(w, smalls, n, count, source, prepare, finish, out_shape, name, micros):
    near = not callable(source)
    group = min(n, 8)
    return pl.pallas_call(
        functools.partial(rows_body, count, n, source, len(smalls), prepare, finish),
        in_specs=[any_spec()] * len(smalls) + [vmem_spec() if near else any_spec()],
        out_specs=vmem_spec(),
        out_shape=jax.ShapeDtypeStruct(out_shape, F32),
        scratch_shapes=small_scratch(smalls)
        + [
            pltpu.VMEM((LANES * group, LANES), F32),
            pltpu.VMEM((LANES * group, LANES), F32),
            pltpu.VMEM((count * LANES, 2 * LANES), BF16),
        ]
        + ([] if near else [pltpu.VMEM((count, LANES, n, LANES), BF16), pltpu.SemaphoreType.DMA((count,))]),
        compiler_params=pltpu.CompilerParams(vmem_limit_bytes=VMEM_LIMIT),
        cost_estimate=cost(micros),
        name=name,
    )(*smalls, w)


def rounded(x):
    return x.astype(BF16).astype(F32)


def orthonormalize_body(tiles, n_basis, got_ref, w_ref, *rest):
    basis, firsts, (v_ref, first_ref, sums_ref) = rest[:n_basis], rest[n_basis : 2 * n_basis], rest[-3:]
    got = jnp.sum(got_ref[...], axis=0)
    sums = jnp.broadcast_to(jnp.sum(got[tiles : tiles + 8], axis=1, keepdims=True), (8, LANES))
    w = w_ref[...]
    first = got[:tiles]
    square = sums[n_basis : n_basis + 1, :]
    for at in range(n_basis):
        h = sums[at : at + 1, :]
        square = square - h * h
        w = w - h * basis[at][...]
        first = first - h * firsts[at][...]
    length = jnp.sqrt(square)
    v_ref[...] = w / length
    first_ref[...] = first / length
    row = lax.broadcasted_iota(jnp.int32, (8, LANES), 0)
    sums_ref[...] = jnp.where(row == n_basis, length, sums)


def orthonormalize(got, w, basis, firsts, tiles):
    return pl.pallas_call(
        functools.partial(orthonormalize_body, tiles, len(basis)),
        in_specs=[vmem_spec()] * (2 + 2 * len(basis)),
        out_specs=[vmem_spec()] * 3,
        out_shape=[
            jax.ShapeDtypeStruct(w.shape, F32),
            jax.ShapeDtypeStruct((tiles, LANES), F32),
            jax.ShapeDtypeStruct((8, LANES), F32),
        ],
        name="orthonormalize",
    )(got, w, *basis, *firsts)


def small_solve(normal_matrix, target):
    size = normal_matrix.shape[0]
    factor = [[None] * size for _ in range(size)]
    for i in range(size):
        for j in range(i + 1):
            value = normal_matrix[i, j]
            for k in range(j):
                value = value - factor[i][k] * factor[j][k]
            factor[i][j] = jnp.sqrt(value) if i == j else value / factor[j][j]
    forward = []
    for i in range(size):
        value = target[i]
        for j in range(i):
            value = value - factor[i][j] * forward[j]
        forward.append(value / factor[i][i])
    backward = [None] * size
    for i in reversed(range(size)):
        value = forward[i]
        for j in range(i + 1, size):
            value = value - factor[j][i] * backward[j]
        backward[i] = value / factor[i][i]
    return backward


def shards(tile_seeds, factors, lower_inverse, upper_inverse, right_side, first_guess):
    n_row = lax.axis_size("row")
    n_col = lax.axis_size("col")
    row_index = lax.axis_index("row")
    col_index = lax.axis_index("col")
    seeds = tile_seeds[:, 0, :, 0]
    n_rows, n_cols = seeds.shape
    order = n_rows * n_row * LANES
    sweeps = lower_inverse.shape[0]
    rows_per = n_rows // sweeps
    cols_per = n_cols // sweeps
    spread = n_row // n_col
    scale = 2.0**-31 * order**-0.5
    has_own = (row_index % n_col == col_index).astype(F32)

    def own(col_part):
        tiles = col_part.reshape(-1, spread, LANES)
        return has_own * lax.dynamic_index_in_dim(tiles, row_index // n_col, 1, keepdims=False)

    def reduce_col(x):
        moved = [lax.ppermute(x, "col", [(i, (i + s) % n_col) for i in range(n_col)]) for s in range(1, n_col)]
        return functools.reduce(jnp.add, moved, x)

    def spread_col(x):
        moved = [lax.ppermute(x, "col", [(i, (i + s) % n_col) for i in range(n_col)]) for s in range(1, n_col)]
        return [x] + moved

    def spread_row(x):
        return lax.all_to_all(x, "row", 0, 0)

    j_index = jnp.arange(LANES, dtype=jnp.int32)
    table = (j_index[None, :] * LANES + j_index[:, None]) * 1640531527

    def finish(y, z):
        part = (y[0] + y[1]).reshape(n_rows, LANES)
        return part * scale + DIAG_SHIFT * own(z)

    def flat(inverse):
        return [inverse[k].reshape(cols_per, LANES * rows_per, LANES) for k in range(sweeps)]

    lower_flat, upper_flat = flat(lower_inverse), flat(upper_inverse)
    place = jnp.stack([row_index // n_col, (row_index % n_col == col_index).astype(jnp.int32)]).astype(jnp.int32)

    def copies(out_ref, rows, *smalls):
        for r in range(n_row):
            for at, row in enumerate(rows):
                out_ref[r, at : at + 1, :] = row

    def inverse_product(inverse, k, smalls, prepare, name):
        return rows_product(
            inverse[k],
            smalls,
            rows_per,
            cols_per,
            None,
            prepare,
            copies,
            (n_row, cols_per, LANES),
            name,
            3.0,
        )

    def factor_product(k, first, solved, extras, signs, micros):
        n_parts = len(solved)

        def prepare(*smalls):
            vecs = []
            for ref in smalls[:n_parts]:
                vecs.append(rounded(ref[...] if len(ref.shape) == 2 else jnp.sum(ref[...], axis=0)))
            return vecs[0] if n_parts == 1 else jnp.concatenate(vecs, axis=0)

        def finish(out_ref, rows, *smalls):
            for at, row in enumerate(rows):
                total = signs[-1] * row
                for sign, ref in zip(signs, smalls[n_parts:]):
                    total = total + sign * ref[at : at + 1, :]
                out_ref[at : at + 1, :] = total

        return rows_product(
            factors,
            list(solved) + list(extras),
            n_parts * cols_per,
            rows_per,
            lambda w, at: w.at[k * rows_per + at, :, pl.ds(first * cols_per, n_parts * cols_per), :],
            prepare,
            finish,
            (rows_per, LANES),
            "factors",
            micros,
        )

    def sums_rows(basis, w):
        rows = [jnp.sum(v * w, axis=0, keepdims=True) for v in basis + [w]]
        return jnp.concatenate(rows + [jnp.zeros((8 - len(rows), LANES), F32)], axis=0)

    def first_product(w, basis):
        n_basis = len(basis)

        def prepare(w_ref, *_):
            return w_ref[0:rows_per, :]

        def finish(out_ref, rows, w_ref, *basis_refs):
            tail = sums_rows([ref[...] for ref in basis_refs], w_ref[...])
            copies(out_ref, rows)
            for r in range(n_row):
                out_ref[r, cols_per:, :] = tail

        return rows_product(
            lower_flat[0],
            [w] + basis,
            rows_per,
            cols_per,
            None,
            prepare,
            finish,
            (n_row, cols_per + 8, LANES),
            "lower_inverse",
            3.0,
        )

    def added(parts):
        return functools.reduce(jnp.add, parts)

    matrix, y = generate(seeds, table, first_guess)
    w = right_side - reduce_col(finish(y, first_guess))
    basis, firsts, directions, columns = [], [], [], []
    for column in range(ITERS):
        got = spread_row(first_product(w, basis))
        vector, first, sums = orthonormalize(got, w, basis, firsts, cols_per)
        columns.append(sums)
        basis.append(vector)
        firsts.append(first)
        solved = [first]
        early = None
        for k in range(1, sweeps):
            if early is None:
                part = factor_product(k, k - 1, solved[k - 1 :], [], [1.0], 3.0)
            else:
                part = factor_product(k, k - 1, solved[k - 1 :], [early], [1.0, 1.0], 3.0)
            parts = spread_col(part)

            def prepare(v_ref, *part_refs, k=k):
                return rounded(v_ref[k * rows_per : (k + 1) * rows_per, :] - added([ref[...] for ref in part_refs]))

            product = inverse_product(lower_flat, k, [vector] + parts, prepare, "lower_inverse")
            product, solved = lax.optimization_barrier((product, solved))
            got = spread_row(product)
            if k + 1 < sweeps:
                early = factor_product(k + 1, 0, solved, [], [1.0], 2.0 * k + 1.0)
            solved.append(got)
        lowered = [own(first)] + [own(jnp.sum(got, axis=0)) for got in solved[1:]]
        solved = [None] * sweeps
        owns = [None] * sweeps
        early = None
        mapped = []
        for k in reversed(range(sweeps)):
            if k == sweeps - 1:
                part = lowered[k]
            elif early is None:
                part = factor_product(k, k + 1, solved[k + 1 : k + 2], [lowered[k]], [1.0, -1.0], 3.0)
            else:
                part = factor_product(k, k + 1, solved[k + 1 : k + 2], [lowered[k], early], [1.0, -1.0, -1.0], 3.0)
            if 0 < k < sweeps - 1:
                part, later = lax.optimization_barrier((part, solved[k + 1 :]))
                parts = spread_col(part)
                early = factor_product(k - 1, k + 1, later, [], [1.0], 2.0 * (sweeps - 1 - k) + 1.0)
                parts, early = lax.optimization_barrier((parts, early))
            else:
                parts = spread_col(part)

            def prepare(*part_refs):
                return rounded(added([ref[...] for ref in part_refs]))

            product = inverse_product(upper_flat, k, parts, prepare, "upper_inverse")
            if k < sweeps - 1:
                product, later = lax.optimization_barrier((product, solved[k + 1]))
                got = spread_row(product)
                mapped = [apply_block(matrix, later, k + 1, sweeps, mapped, [], place, scale)]
                owns[k + 1] = own(jnp.sum(later, axis=0))
                solved[k] = got
            else:
                solved[k] = spread_row(product)
        part = apply_block(matrix, solved[0], 0, sweeps, mapped, owns[1:], place, scale)
        directions.append(jnp.concatenate([jnp.sum(got, axis=0) for got in solved], axis=0))
        w = added(spread_col(part))
    got = spread_row(jnp.broadcast_to(sums_rows(basis, w)[None], (n_row, 8, LANES)))
    sums = jnp.sum(got, axis=(0, 2))
    lengths = [columns[k][k, 0] for k in range(ITERS)]
    initial_norm = lengths[0]
    heights = [[columns[k][j, 0] for j in range(k)] + [lengths[k]] for k in range(1, ITERS)]
    last = [sums[j] for j in range(ITERS)]
    heights.append(last + [jnp.sqrt(functools.reduce(lambda a, h: a - h * h, last, sums[ITERS]))])
    zero = jnp.zeros((), F32)
    hessenberg = jnp.stack([jnp.stack(c + [zero] * (ITERS + 1 - len(c))) for c in heights], axis=1)
    normal_matrix = jnp.dot(hessenberg.T, hessenberg, precision=lax.Precision.HIGHEST)
    weights = small_solve(normal_matrix, initial_norm * hessenberg[0])
    solution = first_guess
    for position in range(ITERS):
        solution = solution + weights[position] * directions[position]
    return (solution, hessenberg)


def solution(mesh):
    in_specs = (
        P(None, "row", None, "col"),
        P(None, "row", None, "col"),
        P(None, None, "col", None, "row"),
        P(None, None, "col", None, "row"),
        P(None, "row"),
        P(None, "col"),
    )
    out_specs = (P(None, "col"), P())
    return jax.shard_map(shards, mesh=mesh, in_specs=in_specs, out_specs=out_specs, check_vma=False)
```

time: 2360 us -> 694 us (0.29)
  matrix products: 827 us -> 0.13 us
  blocking collectives: 695 us -> 13 us
  other arithmetic: 341 us -> 10.6 us
  Pallas kernels: 0 us -> 327 us
  local copies, waits for them, and re-layouts: 372 us -> 47.1 us
  starting transfers between devices: 0 us -> 146 us
  waiting for transfers between devices: 0 us -> 125 us
  loops' own time: 92.1 us -> 0 us
    dot_general x170 -> x0, matrix products: 827 us -> none  [the longest x128 681 us: one_row(): jnp.einsum('icj,cj->i', values, vector_col, precision=lax.Precision.HIGHEST)]
    psum x50 -> x0, blocking collectives: 678 us -> none  [the longest x12 221 us: upper_sweep(): solved[sweep_step] = lax.psum(mapped, 'row')]
    pallas_call x0 -> x70, Pallas kernels: none -> 327 us  [the longest x54 162 us: rows_product(): pl.pallas_call(functools.partial(rows_body, count, n, source, len(smalls)...]
    add x384 -> x3, other arithmetic: 319 us -> 0.02 us  [the longest x2 0.01 us: added(): return functools.reduce(jnp.add, parts)]
    slice x17 -> x6, local copies, waits for them, and re-layouts: 113 us -> 5.74 us  [the longest x2 2.74 us: shards(): columns[k][j, 0]]
    all_to_all x0 -> x24, starting transfers between devices: none -> 104 us  [spread_row(): return lax.all_to_all(x, 'row', 0, 0)]
    another operation x4 -> x0, loops' own time: 92.1 us -> none  [matrix_part(): lax.map(one_row, (seed_grid, jnp.arange(seed_grid.shape[0], dtype=jnp.int...]
    add x128 -> x0, local copies, waits for them, and re-layouts: 89.3 us -> none  [scrambled(): hashed = tile_seed + flat_index * 1640531527]
  transfers between devices with their start and end apart: 0 -> 99, of which waited for: 0 -> 58; matrix products, arithmetic and copies ran while one was open for 0% -> 5% of each run, Pallas kernels for 0% -> 14%
where the time goes in v1:
time: 694 us; the launch traced here: 683 us
  Pallas kernels  327 us (47%)
  starting transfers between devices  146 us (21%)
  waiting for transfers between devices  125 us (18%)
  local copies, waits for them, and re-layouts  47.1 us (7%)
  between operations  13.3 us (2%)
  blocking collectives  13 us (2%)
  other arithmetic  10.6 us (2%)
    pallas_call x54, Pallas kernels, rows_product(): pl.pallas_call(functools.partial(rows_body, count, n, source, len(smalls)...  162 us
    all_to_all x24, starting transfers between devices, spread_row(): return lax.all_to_all(x, 'row', 0, 0)  104 us
    pallas_call x12, Pallas kernels, apply_block(): pl.pallas_call(functools.partial(apply_body, span // chunk, block, slots,...  84.6 us
    pallas_call x1, Pallas kernels, generate(): pl.pallas_call(functools.partial(generate_body, n_rows), grid=(n_cols //...  76.2 us
    all_to_all x24, waiting for transfers between devices, spread_row(): return lax.all_to_all(x, 'row', 0, 0)  75.4 us
    ppermute x72, waiting for transfers between devices, spread_col(): lax.ppermute(x, 'col', [(i, (i + s) % n_col) for i in range(n_col)])  49.4 us
    ppermute x72, starting transfers between devices, spread_col(): lax.ppermute(x, 'col', [(i, (i + s) % n_col) for i in range(n_col)])  39.3 us
    another operation x2, local copies, waits for them, and re-layouts, flat(): inverse[k].reshape(cols_per, LANES * rows_per, LANES)  23.3 us
  transfers between devices with their start and end apart: 99, of which 58 were waited for; matrix products, arithmetic and copies ran while one was open for 5% of the time, Pallas kernels for 14%

profile of v1, /device:TPU:0, one launch (start us, length us, event | category | flops | bytes accessed | tf_op | source)
XLA Modules:
  0.0 682.6 jit_solution(5360159869313282505)
XLA Ops:
  2.2 76.2 %generate.1 = (bf16[8192,4096]{1,0:T(8,128)(2,1)}, f32[16,4096]{1,0:T(8,128)S(1)}) custom-call(s32[32,64]{1,0:T(8,128)S(1)} %bitcast.138, s32[128,128]{1,0:T(8,128)S(1)} %add_multiply_fusion.table, f32[64,128]{1,0:T(8,128)S(1)} %copy-done.32), custom_call_target="tpu_custom_call" | custom-call | tf_op jit(solution)/shard_map/generate/pallas_call | solution.py:63
  82.5 10.9 %slice_bitcast_fusion.4 = (bf16[16,1024,128]{2,1,0:T(8,128)(2,1)}, bf16[16,1024,128]{2,1,0:T(8,128)(2,1)}, bf16[16,1024,128]{2,1,0:T(8,128)(2,1)S(1)}, bf16[16,1024,128]{2,1,0:T(8,128)(2,1)}) fusion(bf16[4,16,128,8,128]{4,3,2,1,0:T(8,128)(2,1)} %param.8), kind=kLoop, calls=%fused_computation.4 | loop fusion | bytes 33554432 | tf_op jit(solution)/shard_map/reshape;squeeze | solution.py:362
  98.2 5.8 all-to-all-start
  104.1 12.4 %slice_bitcast_fusion = (bf16[16,1024,128]{2,1,0:T(8,128)(2,1)}, bf16[16,1024,128]{2,1,0:T(8,128)(2,1)}, bf16[16,1024,128]{2,1,0:T(8,128)(2,1)}, bf16[16,1024,128]{2,1,0:T(8,128)(2,1)}) fusion(bf16[4,16,128,8,128]{4,3,2,1,0:T(8,128)(2,1)} %param.9), kind=kLoop, calls=%fused_computation | loop fusion | bytes 33554432 | tf_op jit(solution)/shard_map/reshape;squeeze | solution.py:362
  131.0 5.7 all-to-all-start.1
  139.5 4.2 all-to-all-done.1.refs_0_.refs_1_
  153.3 3.4 all-to-all-start.2
  156.6 4.2 factors.33.refs_1_
  173.9 3.4 all-to-all-start.3
  177.3 6.9 %all-to-all-done.3 = f32[8,16,128]{2,1,0:T(8,128)S(1)} async-done(((f32[8,16,128]{2,1,0:T(8,128)}), f32[8,16,128]{2,1,0:T(8,128)S(1)}, u32[]{:S(2)}, u32[]{:S(2)}) %all-to-all-start.3) | async-done | bytes 65568 | tf_op jit(solution)/shard_map/all_to_all | solution.py:352
  196.4 6.8 %all-to-all-done.4.refs_0_.refs_1_ = f32[8,16,128]{2,1,0:T(8,128)S(1)} async-done(((f32[8,16,128]{2,1,0:T(8,128)}), f32[8,16,128]{2,1,0:T(8,128)S(1)}, u32[]{:S(2)}, u32[]{:S(2)}) %all-to-all-start.4) | async-done | bytes 65568 | tf_op jit(solution)/shard_map/all_to_all | solution.py:352
  213.5 3.5 all-to-all-start.5
  217.0 7.0 %apply_block.12.refs_1_ = f32[16,4096]{1,0:T(8,128)S(1)} custom-call(s32[2]{0:T(128)S(1)} %pad_add_fusion.place, f32[8,16,128]{2,1,0:T(8,128)S(1)} %all-to-all-done.4.refs_0_.refs_1_, bf16[8192,4096]{1,0:T(8,128)(2,1)} %get-tuple-element.133.refs_1_.refs_2_.refs_5_), custom_call_target="tpu_custom_call" | custom-call | flops 3000000000 | bytes 18000000 | tf_op jit(solution)/shard_map/apply_block/pallas_call | solution.py:162
  229.1 4.3 factors.38.refs_2_
  236.3 5.7 all-to-all-start.6
  242.0 7.0 %apply_block.13.refs_1_ = f32[16,4096]{1,0:T(8,128)S(1)} custom-call(s32[2]{0:T(128)S(1)} %pad_add_fusion.place, f32[8,16,128]{2,1,0:T(8,128)S(1)} %all-to-all-done.5.refs_0_, f32[16,4096]{1,0:T(8,128)S(1)} %apply_block.12.refs_1_, bf16[8192,4096]{1,0:T(8,128)(2,1)} %get-tuple-element.133.refs_1_.refs_2_.refs_5_), custom_call_target="tpu_custom_call" | custom-call | flops 3000000000 | bytes 18000000 | tf_op jit(solution)/shard_map/apply_block/pallas_call | solution.py:162
  260.9 5.7 all-to-all-start.7
  266.7 7.0 %apply_block.14.refs_1_ = f32[16,4096]{1,0:T(8,128)S(1)} custom-call(s32[2]{0:T(128)S(1)} %pad_add_fusion.place, f32[8,16,128]{2,1,0:T(8,128)S(1)} %all-to-all-done.6.refs_0_, f32[16,4096]{1,0:T(8,128)S(1)} %apply_block.13.refs_1_, bf16[8192,4096]{1,0:T(8,128)(2,1)} %get-tuple-element.133.refs_1_.refs_2_.refs_5_), custom_call_target="tpu_custom_call" | custom-call | flops 3000000000 | bytes 18000000 | tf_op jit(solution)/shard_map/apply_block/pallas_call | solution.py:162
  273.7 7.4 %apply_block.15 = f32[32,128]{1,0:T(8,128)S(1)} custom-call(s32[2]{0:T(128)S(1)} %pad_add_fusion.place, f32[8,16,128]{2,1,0:T(8,128)S(1)} %all-to-all-done.7.refs_0_, f32[16,4096]{1,0:T(8,128)S(1)} %apply_block.14.refs_1_, f32[8,128]{1,0:T(8,128)S(1)} %multiply_bitcast_fusion.16.refs_2_, f32[8,128]{1,0:T(8,128)S(1)} %multiply_bitcast_fusion.15.refs_3_, ...), custom_call_target="tpu_custom_call" | custom-call | flops 3000000000 | bytes 18000000 | tf_op jit(solution)/shard_map/apply_block/pallas_call | solution.py:162
  287.4 13.0 %all_to_all.125.got_ref = f32[8,24,128]{2,1,0:T(8,128)} all-to-all(f32[8,24,128]{2,1,0:T(8,128)S(1)} %lower_inverse.16), channel_id=1, replica_groups=mesh['row'=8,'col'=4] {'row'}, dimensions={0} | all-to-all | bytes 196608 | tf_op jit(solution)/shard_map/all_to_all | solution.py:352
  319.1 4.1 all-to-all-done.9.refs_0_.refs_1_
  336.3 4.2 factors.43.refs_1_
  353.5 3.8 all-to-all-start.11
  357.3 6.8 %all-to-all-done.11 = f32[8,16,128]{2,1,0:T(8,128)S(1)} async-done(((f32[8,16,128]{2,1,0:T(8,128)}), f32[8,16,128]{2,1,0:T(8,128)S(1)}, u32[]{:S(2)}, u32[]{:S(2)}) %all-to-all-start.11) | async-done | bytes 65568 | tf_op jit(solution)/shard_map/all_to_all | solution.py:352
  373.1 3.4 all-to-all-start.12
  376.5 6.8 %all-to-all-done.12.refs_0_.refs_1_ = f32[8,16,128]{2,1,0:T(8,128)S(1)} async-done(((f32[8,16,128]{2,1,0:T(8,128)}), f32[8,16,128]{2,1,0:T(8,128)S(1)}, u32[]{:S(2)}, u32[]{:S(2)}) %all-to-all-start.12) | async-done | bytes 65568 | tf_op jit(solution)/shard_map/all_to_all | solution.py:352
  393.4 7.0 %apply_block.16.refs_1_ = f32[16,4096]{1,0:T(8,128)S(1)} custom-call(s32[2]{0:T(128)S(1)} %pad_add_fusion.place, f32[8,16,128]{2,1,0:T(8,128)S(1)} %all-to-all-done.12.refs_0_.refs_1_, bf16[8192,4096]{1,0:T(8,128)(2,1)} %get-tuple-element.133.refs_1_.refs_2_.refs_5_), custom_call_target="tpu_custom_call" | custom-call | flops 3000000000 | bytes 18000000 | tf_op jit(solution)/shard_map/apply_block/pallas_call | solution.py:162
  403.8 7.0 %all-to-all-done.13.refs_0_ = f32[8,16,128]{2,1,0:T(8,128)S(1)} async-done(((f32[8,16,128]{2,1,0:T(8,128)}), f32[8,16,128]{2,1,0:T(8,128)S(1)}, u32[]{:S(2)}, u32[]{:S(2)}) %all-to-all-start.13) | async-done | bytes 65568 | tf_op jit(solution)/shard_map/all_to_all | solution.py:352
  414.9 4.3 factors.48.refs_2_
  425.5 7.0 %apply_block.17.refs_1_ = f32[16,4096]{1,0:T(8,128)S(1)} custom-call(s32[2]{0:T(128)S(1)} %pad_add_fusion.place, f32[8,16,128]{2,1,0:T(8,128)S(1)} %all-to-all-done.13.refs_0_, f32[16,4096]{1,0:T(8,128)S(1)} %apply_block.16.refs_1_, bf16[8192,4096]{1,0:T(8,128)(2,1)} %get-tuple-element.133.refs_1_.refs_2_.refs_5_), custom_call_target="tpu_custom_call" | custom-call | flops 3000000000 | bytes 18000000 | tf_op jit(solution)/shard_map/apply_block/pallas_call | solution.py:162
  444.8 5.7 all-to-all-start.15
  450.4 7.0 %apply_block.18.refs_1_ = f32[16,4096]{1,0:T(8,128)S(1)} custom-call(s32[2]{0:T(128)S(1)} %pad_add_fusion.place, f32[8,16,128]{2,1,0:T(8,128)S(1)} %all-to-all-done.14.refs_0_, f32[16,4096]{1,0:T(8,128)S(1)} %apply_block.17.refs_1_, bf16[8192,4096]{1,0:T(8,128)(2,1)} %get-tuple-element.133.refs_1_.refs_2_.refs_5_), custom_call_target="tpu_custom_call" | custom-call | flops 3000000000 | bytes 18000000 | tf_op jit(solution)/shard_map/apply_block/pallas_call | solution.py:162
  457.5 7.4 %apply_block.19 = f32[32,128]{1,0:T(8,128)S(1)} custom-call(s32[2]{0:T(128)S(1)} %pad_add_fusion.place, f32[8,16,128]{2,1,0:T(8,128)S(1)} %all-to-all-done.15.refs_0_, f32[16,4096]{1,0:T(8,128)S(1)} %apply_block.18.refs_1_, f32[8,128]{1,0:T(8,128)S(1)} %multiply_bitcast_fusion.9.refs_2_, f32[8,128]{1,0:T(8,128)S(1)} %multiply_bitcast_fusion.8.refs_3_, ...), custom_call_target="tpu_custom_call" | custom-call | flops 3000000000 | bytes 18000000 | tf_op jit(solution)/shard_map/apply_block/pallas_call | solution.py:162
  471.9 6.0 all-to-all-start.16
  501.7 4.1 all-to-all-start.17
  508.6 4.1 all-to-all-done.17.refs_0_.refs_1_
  526.4 4.2 factors.53.refs_1_
  547.1 6.9 %all-to-all-done.19 = f32[8,16,128]{2,1,0:T(8,128)S(1)} async-done(((f32[8,16,128]{2,1,0:T(8,128)}), f32[8,16,128]{2,1,0:T(8,128)S(1)}, u32[]{:S(2)}, u32[]{:S(2)}) %all-to-all-start.19) | async-done | bytes 65568 | tf_op jit(solution)/shard_map/all_to_all | solution.py:352
  566.3 6.8 %all-to-all-done.20.refs_0_.refs_1_ = f32[8,16,128]{2,1,0:T(8,128)S(1)} async-done(((f32[8,16,128]{2,1,0:T(8,128)}), f32[8,16,128]{2,1,0:T(8,128)S(1)}, u32[]{:S(2)}, u32[]{:S(2)}) %all-to-all-start.20) | async-done | bytes 65568 | tf_op jit(solution)/shard_map/all_to_all | solution.py:352
  586.7 7.0 %apply_block.20.refs_1_ = f32[16,4096]{1,0:T(8,128)S(1)} custom-call(s32[2]{0:T(128)S(1)} %pad_add_fusion.place, f32[8,16,128]{2,1,0:T(8,128)S(1)} %all-to-all-done.20.refs_0_.refs_1_, bf16[8192,4096]{1,0:T(8,128)(2,1)} %get-tuple-element.133.refs_1_.refs_2_.refs_5_), custom_call_target="tpu_custom_call" | custom-call | flops 3000000000 | bytes 18000000 | tf_op jit(solution)/shard_map/apply_block/pallas_call | solution.py:162
  598.8 4.3 factors.58.refs_2_
  606.0 5.7 all-to-all-start.22
  611.7 7.0 %apply_block.21.refs_1_ = f32[16,4096]{1,0:T(8,128)S(1)} custom-call(s32[2]{0:T(128)S(1)} %pad_add_fusion.place, f32[8,16,128]{2,1,0:T(8,128)S(1)} %all-to-all-done.21.refs_0_, f32[16,4096]{1,0:T(8,128)S(1)} %apply_block.20.refs_1_, bf16[8192,4096]{1,0:T(8,128)(2,1)} %get-tuple-element.133.refs_1_.refs_2_.refs_5_), custom_call_target="tpu_custom_call" | custom-call | flops 3000000000 | bytes 18000000 | tf_op jit(solution)/shard_map/apply_block/pallas_call | solution.py:162
  630.6 5.7 all-to-all-start.23
  636.3 7.0 %apply_block.22.refs_1_ = f32[16,4096]{1,0:T(8,128)S(1)} custom-call(s32[2]{0:T(128)S(1)} %pad_add_fusion.place, f32[8,16,128]{2,1,0:T(8,128)S(1)} %all-to-all-done.22.refs_0_, f32[16,4096]{1,0:T(8,128)S(1)} %apply_block.21.refs_1_, bf16[8192,4096]{1,0:T(8,128)(2,1)} %get-tuple-element.133.refs_1_.refs_2_.refs_5_), custom_call_target="tpu_custom_call" | custom-call | flops 3000000000 | bytes 18000000 | tf_op jit(solution)/shard_map/apply_block/pallas_call | solution.py:162
  643.5 7.0 %apply_block.23 = f32[32,128]{1,0:T(8,128)S(1)} custom-call(s32[2]{0:T(128)S(1)} %pad_add_fusion.place, f32[8,16,128]{2,1,0:T(8,128)S(1)} %all-to-all-done.23.refs_0_, f32[16,4096]{1,0:T(8,128)S(1)} %apply_block.22.refs_1_, f32[8,128]{1,0:T(8,128)S(1)} %multiply_bitcast_fusion.2.refs_2_, f32[8,128]{1,0:T(8,128)S(1)} %multiply_bitcast_fusion.1.refs_3_, ...), custom_call_target="tpu_custom_call" | custom-call | flops 3000000000 | bytes 18000000 | tf_op jit(solution)/shard_map/apply_block/pallas_call | solution.py:162
  655.3 6.0 all-to-all-start.24
  663.2 4.7 all-to-all-done.24
  (449 shorter events, 307.9 us)
Async XLA Ops:
  79.2 14.1 %collective-permute-start.2 = (f32[32,128]{1,0:T(8,128)S(1)}, f32[32,128]{1,0:T(8,128)S(1)}, u32[]{:S(2)}, u32[]{:S(2)}) collective-permute-start(f32[32,128]{1,0:T(8,128)S(1)} %bitcast_add_fusion), channel_id=1, source_target_pairs={{0,3},{1,0},{2,1},{3,2},{4,7},{5,4},{6,5},{7,6},{8,11},{9,8},{10,9... | collective-permute-start | bytes 49160 | tf_op jit(solution)/shard_map/ppermute | solution.py:344
  81.7 11.7 %collective-permute-start.1 = (f32[32,128]{1,0:T(8,128)S(1)}, f32[32,128]{1,0:T(8,128)S(1)}, u32[]{:S(2)}, u32[]{:S(2)}) collective-permute-start(f32[32,128]{1,0:T(8,128)S(1)} %bitcast_add_fusion), channel_id=1, source_target_pairs={{0,2},{1,3},{2,0},{3,1},{4,6},{5,7},{6,4},{7,5},{8,10},{9,11},{10,... | collective-permute-start | bytes 49160 | tf_op jit(solution)/shard_map/ppermute | solution.py:344
  82.3 11.0 %collective-permute-start = (f32[32,128]{1,0:T(8,128)S(1)}, f32[32,128]{1,0:T(8,128)S(1)}, u32[]{:S(2)}, u32[]{:S(2)}) collective-permute-start(f32[32,128]{1,0:T(8,128)S(1)} %bitcast_add_fusion), channel_id=1, source_target_pairs={{0,1},{1,2},{2,3},{3,0},{4,5},{5,6},{6,7},{7,4},{8,9},{9,10},{10,1... | collective-permute-start | bytes 49160 | tf_op jit(solution)/shard_map/ppermute | solution.py:344
  98.2 18.3 %all-to-all-start = ((f32[8,24,128]{2,1,0:T(8,128)}), f32[8,24,128]{2,1,0:T(8,128)S(1)}, u32[]{:S(2)}, u32[]{:S(2)}) async-start(f32[8,24,128]{2,1,0:T(8,128)} %lower_inverse.12), calls=%async_computation | async-start | bytes 196608 | tf_op jit(solution)/shard_map/all_to_all | solution.py:352
  131.0 12.6 %all-to-all-start.1 = ((f32[8,16,128]{2,1,0:T(8,128)}), f32[8,16,128]{2,1,0:T(8,128)S(1)}, u32[]{:S(2)}, u32[]{:S(2)}) async-start(f32[8,16,128]{2,1,0:T(8,128)} %lower_inverse.13), calls=%async_computation.1 | async-start | bytes 131072 | tf_op jit(solution)/shard_map/all_to_all | solution.py:352
  153.3 10.2 %all-to-all-start.2 = ((f32[8,16,128]{2,1,0:T(8,128)}), f32[8,16,128]{2,1,0:T(8,128)S(1)}, u32[]{:S(2)}, u32[]{:S(2)}) async-start(f32[8,16,128]{2,1,0:T(8,128)} %lower_inverse.14), calls=%async_computation.2 | async-start | bytes 131072 | tf_op jit(solution)/shard_map/all_to_all | solution.py:352
  173.9 10.2 %all-to-all-start.3 = ((f32[8,16,128]{2,1,0:T(8,128)}), f32[8,16,128]{2,1,0:T(8,128)S(1)}, u32[]{:S(2)}, u32[]{:S(2)}) async-start(f32[8,16,128]{2,1,0:T(8,128)} %lower_inverse.15), calls=%async_computation.3 | async-start | bytes 131072 | tf_op jit(solution)/shard_map/all_to_all | solution.py:352
  193.0 10.2 %all-to-all-start.4 = ((f32[8,16,128]{2,1,0:T(8,128)}), f32[8,16,128]{2,1,0:T(8,128)S(1)}, u32[]{:S(2)}, u32[]{:S(2)}) async-start(f32[8,16,128]{2,1,0:T(8,128)} %upper_inverse.12), calls=%async_computation.4 | async-start | bytes 131072 | tf_op jit(solution)/shard_map/all_to_all | solution.py:352
  206.0 4.4 collective-permute-start.17
  206.1 4.4 collective-permute-start.16
  213.5 10.5 %all-to-all-start.5 = ((f32[8,16,128]{2,1,0:T(8,128)}), f32[8,16,128]{2,1,0:T(8,128)S(1)}, u32[]{:S(2)}, u32[]{:S(2)}) async-start(f32[8,16,128]{2,1,0:T(8,128)} %upper_inverse.13), calls=%async_computation.5 | async-start | bytes 131072 | tf_op jit(solution)/shard_map/all_to_all | solution.py:352
  226.9 6.5 collective-permute-start.20
  228.5 5.0 collective-permute-start.19
  229.1 4.4 collective-permute-start.18
  236.3 12.8 %all-to-all-start.6 = ((f32[8,16,128]{2,1,0:T(8,128)}), f32[8,16,128]{2,1,0:T(8,128)S(1)}, u32[]{:S(2)}, u32[]{:S(2)}) async-start(f32[8,16,128]{2,1,0:T(8,128)} %upper_inverse.14), calls=%async_computation.6 | async-start | bytes 131072 | tf_op jit(solution)/shard_map/all_to_all | solution.py:352
  260.9 12.8 %all-to-all-start.7 = ((f32[8,16,128]{2,1,0:T(8,128)}), f32[8,16,128]{2,1,0:T(8,128)S(1)}, u32[]{:S(2)}, u32[]{:S(2)}) async-start(f32[8,16,128]{2,1,0:T(8,128)} %upper_inverse.15), calls=%async_computation.7 | async-start | bytes 131072 | tf_op jit(solution)/shard_map/all_to_all | solution.py:352
  281.2 3.9 collective-permute-start.25
  313.0 10.2 %all-to-all-start.9 = ((f32[8,16,128]{2,1,0:T(8,128)}), f32[8,16,128]{2,1,0:T(8,128)S(1)}, u32[]{:S(2)}, u32[]{:S(2)}) async-start(f32[8,16,128]{2,1,0:T(8,128)} %lower_inverse.17), calls=%async_computation.9 | async-start | bytes 131072 | tf_op jit(solution)/shard_map/all_to_all | solution.py:352
  332.9 10.2 %all-to-all-start.10 = ((f32[8,16,128]{2,1,0:T(8,128)}), f32[8,16,128]{2,1,0:T(8,128)S(1)}, u32[]{:S(2)}, u32[]{:S(2)}) async-start(f32[8,16,128]{2,1,0:T(8,128)} %lower_inverse.18), calls=%async_computation.10 | async-start | bytes 131072 | tf_op jit(solution)/shard_map/all_to_all | solution.py:352
  353.5 10.6 %all-to-all-start.11 = ((f32[8,16,128]{2,1,0:T(8,128)}), f32[8,16,128]{2,1,0:T(8,128)S(1)}, u32[]{:S(2)}, u32[]{:S(2)}) async-start(f32[8,16,128]{2,1,0:T(8,128)} %lower_inverse.19), calls=%async_computation.11 | async-start | bytes 131072 | tf_op jit(solution)/shard_map/all_to_all | solution.py:352
  373.1 10.2 %all-to-all-start.12 = ((f32[8,16,128]{2,1,0:T(8,128)}), f32[8,16,128]{2,1,0:T(8,128)S(1)}, u32[]{:S(2)}, u32[]{:S(2)}) async-start(f32[8,16,128]{2,1,0:T(8,128)} %upper_inverse.16), calls=%async_computation.12 | async-start | bytes 131072 | tf_op jit(solution)/shard_map/all_to_all | solution.py:352
  386.1 4.3 collective-permute-start.41
  386.2 4.3 collective-permute-start.40
  400.4 10.4 %all-to-all-start.13 = ((f32[8,16,128]{2,1,0:T(8,128)}), f32[8,16,128]{2,1,0:T(8,128)S(1)}, u32[]{:S(2)}, u32[]{:S(2)}) async-start(f32[8,16,128]{2,1,0:T(8,128)} %upper_inverse.17), calls=%async_computation.13 | async-start | bytes 131072 | tf_op jit(solution)/shard_map/all_to_all | solution.py:352
  413.6 5.6 collective-permute-start.44
  414.4 4.8 collective-permute-start.43
  414.8 4.5 collective-permute-start.42
  422.1 10.4 %all-to-all-start.14 = ((f32[8,16,128]{2,1,0:T(8,128)}), f32[8,16,128]{2,1,0:T(8,128)S(1)}, u32[]{:S(2)}, u32[]{:S(2)}) async-start(f32[8,16,128]{2,1,0:T(8,128)} %upper_inverse.18), calls=%async_computation.14 | async-start | bytes 131072 | tf_op jit(solution)/shard_map/all_to_all | solution.py:352
  444.8 12.7 %all-to-all-start.15 = ((f32[8,16,128]{2,1,0:T(8,128)}), f32[8,16,128]{2,1,0:T(8,128)S(1)}, u32[]{:S(2)}, u32[]{:S(2)}) async-start(f32[8,16,128]{2,1,0:T(8,128)} %upper_inverse.19), calls=%async_computation.15 | async-start | bytes 131072 | tf_op jit(solution)/shard_map/all_to_all | solution.py:352
  465.0 4.0 collective-permute-start.49
  471.9 13.1 %all-to-all-start.16 = ((f32[8,24,128]{2,1,0:T(8,128)}), f32[8,24,128]{2,1,0:T(8,128)S(1)}, u32[]{:S(2)}, u32[]{:S(2)}) async-start(f32[8,24,128]{2,1,0:T(8,128)} %lower_inverse.20), calls=%async_computation.16 | async-start | bytes 196608 | tf_op jit(solution)/shard_map/all_to_all | solution.py:352
  490.7 5.9 collective-permute-start.53
  490.8 5.8 collective-permute-start.52
  492.1 4.5 collective-permute-start.51
  501.7 10.9 %all-to-all-start.17 = ((f32[8,16,128]{2,1,0:T(8,128)}), f32[8,16,128]{2,1,0:T(8,128)S(1)}, u32[]{:S(2)}, u32[]{:S(2)}) async-start(f32[8,16,128]{2,1,0:T(8,128)} %lower_inverse.21), calls=%async_computation.17 | async-start | bytes 131072 | tf_op jit(solution)/shard_map/all_to_all | solution.py:352
  523.1 10.2 %all-to-all-start.18 = ((f32[8,16,128]{2,1,0:T(8,128)}), f32[8,16,128]{2,1,0:T(8,128)S(1)}, u32[]{:S(2)}, u32[]{:S(2)}) async-start(f32[8,16,128]{2,1,0:T(8,128)} %lower_inverse.22), calls=%async_computation.18 | async-start | bytes 131072 | tf_op jit(solution)/shard_map/all_to_all | solution.py:352
  543.8 10.2 %all-to-all-start.19 = ((f32[8,16,128]{2,1,0:T(8,128)}), f32[8,16,128]{2,1,0:T(8,128)S(1)}, u32[]{:S(2)}, u32[]{:S(2)}) async-start(f32[8,16,128]{2,1,0:T(8,128)} %lower_inverse.23), calls=%async_computation.19 | async-start | bytes 131072 | tf_op jit(solution)/shard_map/all_to_all | solution.py:352
  562.9 10.2 %all-to-all-start.20 = ((f32[8,16,128]{2,1,0:T(8,128)}), f32[8,16,128]{2,1,0:T(8,128)S(1)}, u32[]{:S(2)}, u32[]{:S(2)}) async-start(f32[8,16,128]{2,1,0:T(8,128)} %upper_inverse.20), calls=%async_computation.20 | async-start | bytes 131072 | tf_op jit(solution)/shard_map/all_to_all | solution.py:352
  575.9 4.4 collective-permute-start.65
  576.0 4.4 collective-permute-start.64
  583.3 10.4 %all-to-all-start.21 = ((f32[8,16,128]{2,1,0:T(8,128)}), f32[8,16,128]{2,1,0:T(8,128)S(1)}, u32[]{:S(2)}, u32[]{:S(2)}) async-start(f32[8,16,128]{2,1,0:T(8,128)} %upper_inverse.21), calls=%async_computation.21 | async-start | bytes 131072 | tf_op jit(solution)/shard_map/all_to_all | solution.py:352
  596.6 6.5 collective-permute-start.68
  598.1 5.0 collective-permute-start.67
  598.8 4.4 collective-permute-start.66
  606.0 12.8 %all-to-all-start.22 = ((f32[8,16,128]{2,1,0:T(8,128)}), f32[8,16,128]{2,1,0:T(8,128)S(1)}, u32[]{:S(2)}, u32[]{:S(2)}) async-start(f32[8,16,128]{2,1,0:T(8,128)} %upper_inverse.22), calls=%async_computation.22 | async-start | bytes 131072 | tf_op jit(solution)/shard_map/all_to_all | solution.py:352
  630.6 12.9 %all-to-all-start.23 = ((f32[8,16,128]{2,1,0:T(8,128)}), f32[8,16,128]{2,1,0:T(8,128)S(1)}, u32[]{:S(2)}, u32[]{:S(2)}) async-start(f32[8,16,128]{2,1,0:T(8,128)} %upper_inverse.23), calls=%async_computation.23 | async-start | bytes 131072 | tf_op jit(solution)/shard_map/all_to_all | solution.py:352
  650.6 3.9 collective-permute-start.73
  655.3 12.7 %all-to-all-start.24 = ((f32[8,8,128]{2,1,0:T(8,128)}), f32[8,8,128]{2,1,0:T(8,128)S(1)}, u32[]{:S(2)}, u32[]{:S(2)}) async-start(f32[8,8,128]{2,1,0:T(8,128)} %broadcast_in_dim.28), calls=%async_computation.24 | async-start | bytes 65536 | tf_op jit(solution)/shard_map/all_to_all | solution.py:352
  (114 other events, 975.7 us)
